TPU v7x, 32 devices: a 4x4x1 block of a 4x4x8 slice. The times are simulated.
32 devices in a mesh: dp: 1 (over z), ep: 32 (over y, x, core).
Axes of the slice: x: 4, y: 4, z: 1, core: 2. Of those that a mesh axis runs over, the one named last changes fastest.
The devices are a block of a 4x4x8 slice.
Arguments:
- x_tok: bfloat16 [16384, 2048], P(('dp', 'ep'))
- topk_idx: int32 [16384, 6], P(('dp', 'ep'))
- topk_w: float32 [16384, 6], P(('dp', 'ep'))
- w_in: bfloat16 [64, 2048, 1408], P('ep')
- w_out: bfloat16 [64, 1408, 2048], P('ep')
- shared_in: bfloat16 [2048, 2816], replicated
- shared_out: bfloat16 [2816, 2048], replicated
Outputs:
- output: bfloat16 [16384, 2048], P(('dp', 'ep'))
All inputs are finite; a program needn't handle non-finite values.
Results may differ from a plain program's by a relative error of at most 0.001.
Values are sent between devices in bfloat16 or wider.
A program may use at most 768 MiB of HBM per device.

v0:
```python
import functools
import math

import jax
import jax.numpy as jnp
from jax import lax
from jax.experimental import pallas as pl
from jax.experimental.pallas import tpu as pltpu
from jax.sharding import PartitionSpec as P


LOAD_MULT = 3
BASE_CAP = 48
HOT_STATIC = 2
SRC_BLOCK = 8
COMBINE_BLOCK = 512
EXTRA_ROWS = 16
VMEM = 60 * 2 ** 20


def gelu(z):
    return jax.nn.gelu(z, approximate=True)


def gather_rows(slot_ref, x_ref, cap, put):
    groups, blk, toks = slot_ref.shape
    slot_iota = lax.broadcasted_iota(jnp.int32, (cap, toks), 0)

    def one(s, carry):
        picks = [(slot_iota == slot_ref[g, pl.ds(s, 1), :]).astype(jnp.bfloat16) for g in range(groups)]
        pick = jnp.concatenate(picks, axis=0) if groups > 1 else picks[0]
        got = jnp.dot(pick, x_ref[s], preferred_element_type=jnp.float32).astype(jnp.bfloat16)
        for g in range(groups):
            put(g, pl.ds(pl.multiple_of(s * cap, 16), cap), got[g * cap:(g + 1) * cap])
        return carry

    lax.fori_loop(0, blk, one, 0)


def first_kernel(cap, sel_ref, slot_ref, x_ref, w_ref, acc_ref, rows_ref):
    def put(g, where, rows):
        rows_ref[g, where, :] = rows

    gather_rows(slot_ref, x_ref, cap, put)
    for g in range(w_ref.shape[0]):
        acc_ref[g] = jnp.dot(rows_ref[g], w_ref[g], preferred_element_type=jnp.float32)


def second_kernel(cap, sel_ref, slot_ref, x_ref, acc_ref, w_ref, v_ref, out_ref, rows_ref):
    def put(g, where, rows):
        rows_ref[g, where, :] = rows

    gather_rows(slot_ref, x_ref, cap, put)
    for g in range(w_ref.shape[0]):
        pre = acc_ref[g] + jnp.dot(rows_ref[g], w_ref[g], preferred_element_type=jnp.float32)
        hid = gelu(pre).astype(jnp.bfloat16)
        out = jnp.dot(hid, v_ref[g], preferred_element_type=jnp.float32).astype(jnp.bfloat16)
        out_ref[:, g * cap:(g + 1) * cap] = out.reshape(out_ref.shape[0], cap, out_ref.shape[2])


def combine_kernel(comb_ref, back_ref, part_ref, out_ref):
    routed = jnp.dot(comb_ref[...], back_ref[...], preferred_element_type=jnp.float32)
    out_ref[...] = (part_ref[...] + routed).astype(out_ref.dtype)


def params():
    return pltpu.CompilerParams(dimension_semantics=("arbitrary",), vmem_limit_bytes=VMEM)


def cost(flops, nbytes, trans=0):
    return pl.CostEstimate(flops=int(flops), bytes_accessed=int(nbytes), transcendentals=int(trans))


def once(shape, index):
    return pl.BlockSpec(shape, index, pipeline_mode=pl.Buffered(1))


def expert_first(sel, slots, x_part, w_in, cap):
    groups, srcs, toks = slots.shape
    width, ff, blk = x_part.shape[2], w_in.shape[2], SRC_BLOCK
    return pl.pallas_call(
        functools.partial(first_kernel, cap),
        out_shape=jax.ShapeDtypeStruct((groups, srcs * cap, ff), jnp.float32),
        grid_spec=pltpu.PrefetchScalarGridSpec(
            num_scalar_prefetch=1,
            grid=(srcs // blk,),
            in_specs=[
                pl.BlockSpec((groups, blk, toks), lambda i, sel: (0, i, 0)),
                pl.BlockSpec((blk, toks, width), lambda i, sel: (i, 0, 0)),
                once((groups, width, ff), lambda i, sel: (sel[0], 0, 0)),
            ],
            out_specs=pl.BlockSpec((groups, blk * cap, ff), lambda i, sel: (0, i, 0)),
            scratch_shapes=[pltpu.VMEM((groups, blk * cap, width), jnp.bfloat16)],
        ),
        compiler_params=params(),
        cost_estimate=cost(2 * groups * srcs * cap * width * (ff + toks),
                           srcs * toks * width * 2 + groups * (width * ff * 2 + srcs * cap * ff * 4)),
        name="expert_first",
    )(sel, slots, x_part, w_in)


def expert_second(sel, slots, x_part, acc, w_in, w_out, cap):
    groups, srcs, toks = slots.shape
    width, ff, model, blk = x_part.shape[2], w_out.shape[1], w_out.shape[2], SRC_BLOCK
    last = w_in.shape[1] // width - 1
    return pl.pallas_call(
        functools.partial(second_kernel, cap),
        out_shape=jax.ShapeDtypeStruct((srcs, groups * cap, model), jnp.bfloat16),
        grid_spec=pltpu.PrefetchScalarGridSpec(
            num_scalar_prefetch=1,
            grid=(srcs // blk,),
            in_specs=[
                pl.BlockSpec((groups, blk, toks), lambda i, sel: (0, i, 0)),
                pl.BlockSpec((blk, toks, width), lambda i, sel: (i, 0, 0)),
                pl.BlockSpec((groups, blk * cap, ff), lambda i, sel: (0, i, 0)),
                once((groups, width, ff), lambda i, sel: (sel[0], last, 0)),
                once((groups, ff, model), lambda i, sel: (sel[0], 0, 0)),
            ],
            out_specs=pl.BlockSpec((blk, groups * cap, model), lambda i, sel: (i, 0, 0)),
            scratch_shapes=[pltpu.VMEM((groups, blk * cap, width), jnp.bfloat16)],
        ),
        compiler_params=params(),
        cost_estimate=cost(2 * groups * srcs * cap * (width * (ff + toks) + ff * model),
                           srcs * toks * width * 2 + groups * ((width + model) * ff * 2 + srcs * cap * (ff * 4 + model * 2)),
                           groups * srcs * cap * ff),
        name="expert_second",
    )(sel, slots, x_part, acc, w_in, w_out)


def combine(comb, back, part):
    toks, pairs = comb.shape
    model, blk = back.shape[1], COMBINE_BLOCK
    return pl.pallas_call(
        combine_kernel,
        out_shape=jax.ShapeDtypeStruct((toks, model), jnp.bfloat16),
        grid=(model // blk,),
        in_specs=[
            once((toks, pairs), lambda i: (0, 0)),
            pl.BlockSpec((pairs, blk), lambda i: (0, i)),
            pl.BlockSpec((toks, blk), lambda i: (0, i)),
        ],
        out_specs=pl.BlockSpec((toks, blk), lambda i: (0, i)),
        compiler_params=params(),
        cost_estimate=cost(2 * toks * pairs * model, pairs * (toks + model) * 2 + toks * model * 6),
        name="combine",
    )(comb, back, part)


def scatter_kernel(owner, axis, size, rows_ref, out_ref, local_sem, send_sem, recv_sem):
    me = lax.axis_index(axis)
    barrier = pltpu.get_barrier_semaphore()
    stride = next(n for n in range(size // 3 | 1, 2 * size) if math.gcd(n, size) == 1)

    def send_to(k):
        dst = lax.rem(owner + k * stride, size)
        return pltpu.make_async_remote_copy(
            src_ref=rows_ref.at[dst], dst_ref=out_ref, send_sem=send_sem.at[k], recv_sem=recv_sem,
            device_id={axis: dst}, device_id_type=pl.DeviceIdType.MESH)

    @pl.when(me != owner)
    def _():
        pl.semaphore_signal(barrier, inc=1, device_id={axis: owner}, device_id_type=pl.DeviceIdType.MESH)
        send_to(0).wait_recv()

    @pl.when(me == owner)
    def _():
        own = pltpu.make_async_copy(rows_ref.at[owner], out_ref, local_sem)
        own.start()
        pl.semaphore_wait(barrier, size - 1)
        lax.fori_loop(1, size, lambda k, c: (send_to(k).start(), c)[1], 0)
        lax.fori_loop(1, size, lambda k, c: (send_to(k).wait_send(), c)[1], 0)
        own.wait()


def scatter_from(owner, axis, size, ident, rows):
    return pl.pallas_call(
        functools.partial(scatter_kernel, owner, axis, size),
        out_shape=jax.ShapeDtypeStruct(rows.shape[1:], rows.dtype),
        in_specs=[pl.BlockSpec(memory_space=pltpu.VMEM)],
        out_specs=pl.BlockSpec(memory_space=pl.ANY),
        scratch_shapes=[pltpu.SemaphoreType.DMA, pltpu.SemaphoreType.DMA((size,)), pltpu.SemaphoreType.DMA],
        compiler_params=pltpu.CompilerParams(collective_id=ident, has_side_effects=True, vmem_limit_bytes=32 * 2 ** 20),
        name="scatter_over",
    )(rows)


def solution(mesh):
    group_size = mesh.shape['ep']

    def local_layer(x_loc, idx_loc, gate_loc, w_in, w_out, shared_in, shared_out):
        tok_rows, top_k = idx_loc.shape
        model = x_loc.shape[1]
        own = w_in.shape[0]
        num_experts = own * group_size
        slot_cap = min(tok_rows, LOAD_MULT * tok_rows * top_k // num_experts)
        cap = BASE_CAP
        over_cap = slot_cap - cap
        cut = model * 3 // 4
        me = lax.axis_index('ep')
        experts = jnp.arange(num_experts, dtype=jnp.int32)

        before = (lax.broadcasted_iota(jnp.int32, (tok_rows, tok_rows), 0)
                  <= lax.broadcasted_iota(jnp.int32, (tok_rows, tok_rows), 1)).astype(jnp.bfloat16)

        def slots_of(hit):
            count = jnp.dot(hit.reshape(-1, tok_rows).astype(jnp.bfloat16), before, preferred_element_type=jnp.float32)
            return jnp.where(hit, count.reshape(hit.shape).astype(jnp.int32) - 1, -1)

        idx_t = idx_loc.T
        count_loc = jnp.sum((idx_t.reshape(1, -1) == experts[:, None]).astype(jnp.int32), axis=1)
        meta = jnp.concatenate([idx_t, jnp.pad(count_loc[None], ((0, 0), (0, tok_rows - num_experts)))], axis=0)
        meta = jnp.pad(meta.astype(jnp.bfloat16), ((0, EXTRA_ROWS - top_k - 1), (0, cut - tok_rows)))
        x_first = lax.all_gather(jnp.concatenate([x_loc[:, :cut], meta], axis=0), 'ep')
        x_second = lax.all_gather(x_loc[:, cut:], 'ep')

        gate_t = gate_loc.astype(jnp.bfloat16).T
        same = idx_t[None] == experts[:, None, None]
        hit_loc = jnp.any(same, axis=1)
        gate_of = jnp.sum(jnp.where(same, gate_t[None], 0).astype(jnp.float32), axis=1).astype(jnp.bfloat16)
        slot_loc = slots_of(hit_loc)

        pick = slot_loc[:, None, :] == jnp.arange(cap, dtype=jnp.int32)[None, :, None]
        comb = jnp.where(pick, gate_of[:, None, :], 0).astype(jnp.bfloat16).reshape(num_experts * cap, tok_rows).T

        def weigh(comb, rows):
            return lax.dot_general(comb, rows, (((0,), (0,)), ((), ())), preferred_element_type=jnp.float32)

        shared_hidden = gelu(jnp.dot(x_loc, shared_in, preferred_element_type=jnp.float32)).astype(jnp.bfloat16)
        shared_val = jnp.dot(shared_hidden, shared_out, preferred_element_type=jnp.float32)
        x_first, shared_val, comb = lax.optimization_barrier((x_first, shared_val, comb))

        idx_all = x_first[:, tok_rows:tok_rows + top_k, :tok_rows].astype(jnp.int32)
        load = jnp.max(x_first[:, tok_rows + top_k, :num_experts].astype(jnp.int32), axis=0)

        def slots_all(expert):
            return slots_of(jnp.any(idx_all == expert, axis=1))

        over = load > cap
        over_rank = jnp.sum((over[None, :] & (experts[None, :] < experts[:, None])).astype(jnp.int32), axis=1)
        num_over = jnp.sum(over.astype(jnp.int32))

        def over_expert(i):
            chosen = over & (over_rank == i)
            return jnp.where(i < num_over, jnp.sum(jnp.where(chosen, experts, 0)), num_experts)

        def over_setup(i):
            expert = over_expert(i)
            mine = expert // own == me
            return expert, mine, jnp.where(mine, expert % own, 0).reshape(1), (slots_all(expert) - cap)[None]

        def over_first(setup, x_part):
            _, mine, sel, slots = setup
            return lax.cond(
                mine, lambda: expert_first(sel, slots, x_part, w_in, over_cap),
                lambda: jnp.zeros((1, group_size * over_cap, w_in.shape[2]), jnp.float32))

        def over_second(setup, x_part, acc):
            _, mine, sel, slots = setup
            return lax.cond(
                mine, lambda: expert_second(sel, slots, x_part, acc, w_in, w_out, over_cap),
                lambda: jnp.zeros((group_size, over_cap, model), jnp.bfloat16))

        base_sel = jnp.zeros((1,), jnp.int32)
        base_slots = jnp.stack([slots_all(me * own + g) for g in range(own)])
        acc = expert_first(base_sel, base_slots, x_first, w_in, cap)
        setups = [over_setup(i) for i in range(HOT_STATIC)]
        over_accs = [over_first(setup, x_first) for setup in setups]
        x_second, acc, over_accs = lax.optimization_barrier((x_second, acc, over_accs))
        out = expert_second(base_sel, base_slots, x_second, acc, w_in, w_out, cap)
        back = lax.all_to_all(out, 'ep', 0, 0, tiled=True).reshape(num_experts * cap, model)
        x_over, over_accs, _ = lax.optimization_barrier((x_second, over_accs, out))
        over_outs = [over_second(s, x_over, a) for s, a in zip(setups, over_accs)]
        over_outs = lax.optimization_barrier(over_outs)

        def over_combine(expert, rows):
            at = jnp.minimum(expert, num_experts - 1)
            slot = lax.dynamic_index_in_dim(slot_loc, at, 0, keepdims=True)
            gate = lax.dynamic_index_in_dim(gate_of, at, 0, keepdims=True)
            pick = (slot - cap == lax.broadcasted_iota(jnp.int32, (over_cap, tok_rows), 0)) & (expert < num_experts)
            return weigh(jnp.where(pick, gate, 0).astype(jnp.bfloat16), rows)

        def scatter(setup, rows):
            owner = jnp.minimum(setup[0], num_experts - 1) // own
            return lax.switch(owner, [functools.partial(scatter_from, d, 'ep', group_size, 0) for d in range(group_size)], rows)

        def spread(rows):
            return lax.psum_scatter(rows.reshape(group_size * over_cap, model), 'ep', scatter_dimension=0, tiled=True)

        rest = [spread(rows) for rows in over_outs[1:]]
        total = shared_val + over_combine(setups[0][0], scatter(setups[0], over_outs[0]))
        for setup, rows in zip(setups[1:], rest):
            total = total + over_combine(setup[0], rows)

        def more(i, total):
            setup = over_setup(i)
            return total + over_combine(setup[0], spread(over_second(setup, x_over, over_first(setup, x_first))))

        total = lax.fori_loop(HOT_STATIC, jnp.maximum(num_over, HOT_STATIC), more, total)
        return combine(comb, back, total)

    tok_spec = P(('dp', 'ep'), None)
    expert_spec = P('ep', None, None)
    whole_spec = P(None, None)
    return jax.shard_map(local_layer, mesh=mesh, in_specs=(tok_spec, tok_spec, tok_spec, expert_spec, expert_spec, whole_spec, whole_spec), out_specs=tok_spec, check_vma=False)
```

profile of v0, /device:TPU:111, one launch (start us, length us, event | category | flops | bytes accessed | tf_op | source)
XLA Modules:
  0.0 695.8 jit_solution(2674895503996267812)
XLA Ops:
  6.6 0.0 all-gather.5.cloned.1.call-start
  6.6 0.8 bitcast_convert_fusion
  7.3 0.7 eq.174
  8.1 0.2 convert_reduce_fusion
  8.3 1.5 slice.12
  9.8 1.3 fusion.35
  11.1 0.1 all-gather.5.cloned.1.call-update
  11.1 0.1 all-gather.7.cloned.1.call-start
  11.2 1.9 slice.14
  13.0 0.1 all-gather.7.cloned.1.call-update
  13.1 0.1 reduce-scatter.3.cloned.1.call-start
  13.2 0.0 copy-done.6
  13.2 0.0 copy-done.2
  13.2 0.1 fusion.58
  13.3 0.0 copy-start.1
  13.3 0.6 copy-done.1
  13.9 0.2 broadcast_in_dim.127
  14.2 3.1 copy.13
  17.3 0.1 fusion.53
  17.4 0.2 fusion.37
  17.6 0.0 copy-start.3
  17.6 3.5 eq.181
  21.1 0.0 copy-done.3
  21.1 7.5 %copy.12 = s32[3072,512]{0,1:T(8,128)} copy(s32[3072,512]{1,0:T(8,128)} %bitcast.64) | data formatting | bytes 12582912 | tf_op jit(solution)/shard_map/eq | solution.py:222
  28.6 0.1 eq.184
  28.7 0.0 copy-done
  28.7 5.3 fusion.28.comb_ref
  33.9 22.7 %fusion.29 = f32[512,2048]{1,0:T(8,128)} fusion(bf16[2816,2048]{1,0:T(8,128)(2,1)} %param.59, bf16[512,2048]{1,0:T(8,128)(2,1)} %param.53, bf16[2048,2816]{1,0:T(8,128)(2,1)} %param.58), kind=kOutput, calls=%fused_computation.37 | convolution fusion | flops 11824136192 | bytes 29360128 | tf_op jit(solution)/shard_map/dot_general | solution.py:229
  56.7 111.4 %all-gather.5.cloned.1.call-done = bf16[16896,1536]{1,0:T(8,128)(2,1)} async-done(((bf16[528,1536]{1,0:T(8,128)(2,1)}), bf16[16896,1536]{1,0:T(8,128)(2,1)}) %all-gather.5.cloned.1.call-update) | async-done | bytes 51904528 | tf_op jit(solution)/shard_map/all_gather | solution.py:213
  168.1 0.9 convert_reduce_fusion.2
  169.0 0.0 copy-start.7
  169.0 0.1 convert_reduce_fusion.1
  169.1 0.0 copy-start.4
  169.1 0.6 copy-done.4
  169.7 0.7 fusion.78
  170.4 0.0 copy-done.7
  173.2 1.7 fusion.57
  174.9 0.2 fusion.49
  175.1 0.2 fusion.51
  175.3 7.7 %conditional.7 = (f32[1,3072,1408]{2,1,0:T(8,128)}) conditional(s32[]{:T(128)} %convert_element_type.95, () %tuple.157, (s32[1]{0:T(128)}, s32[1,32,512]{2,1,0:T(8,128)S(1)}, bf16[32,528,1536]{2,1,0:T(8,128)(2,1)}, bf16[2,2048,1408]{2,1,0:T(8,128)(2,1)}) %tuple.254), branch_computations={%region_10.11_spmd, %region_11.12_spmd} | conditional | flops 18119393280 | bytes 71958536 | solution.py:253
  175.3 7.5 %broadcast.69 = f32[1,3072,1408]{2,1,0:T(8,128)} broadcast(f32[]{:T(128)} %constant.170.clone), dimensions={} | broadcast | bytes 17301508 | tf_op jit(solution)/shard_map/broadcast.4
  183.0 7.1 %conditional.8 = (f32[1,3072,1408]{2,1,0:T(8,128)}) conditional(s32[]{:T(128)} %convert_element_type.97, () %tuple.159, (s32[1]{0:T(128)}, s32[1,32,512]{2,1,0:T(8,128)S(1)}, bf16[32,528,1536]{2,1,0:T(8,128)(2,1)}, bf16[2,2048,1408]{2,1,0:T(8,128)(2,1)}) %tuple.255), branch_computations={%region_14.15_spmd, %region_15.16_spmd} | conditional | flops 18119393280 | bytes 71958536 | solution.py:253
  183.0 7.1 %broadcast.70 = f32[1,3072,1408]{2,1,0:T(8,128)} broadcast(f32[]{:T(128)} %constant.171.clone), dimensions={} | broadcast | bytes 17301508 | tf_op jit(solution)/shard_map/broadcast.6
  190.1 0.2 fusion.44
  190.3 0.2 fusion.47
  190.5 0.7 pad_add_fusion.slot_ref
  191.1 36.8 %expert_first.7.acc_ref = f32[2,1536,1408]{2,1,0:T(8,128)} custom-call(s32[1]{0:T(128)} %constant.193.clone.1.sel_ref, s32[2,32,512]{2,1,0:T(8,128)} %pad_add_fusion.slot_ref, bf16[32,528,1536]{2,1,0:T(8,128)(2,1)} %bitcast.59, bf16[2,2048,1408]{2,1,0:T(8,128)(2,1)} %w_ref.3), custom_call_target="tpu_custom_call" | custom-call | flops 18119393280 | bytes 76283904 | tf_op jit(solution)/shard_map/expert_first/pallas_call | solution.py:81
  227.9 9.1 %all-gather.7.cloned.1.call-done = bf16[16384,512]{1,0:T(8,128)(2,1)} async-done(((bf16[512,512]{1,0:T(8,128)(2,1)}), bf16[16384,512]{1,0:T(8,128)(2,1)}) %all-gather.7.cloned.1.call-update) | async-done | bytes 16777232 | tf_op jit(solution)/shard_map/all_gather | solution.py:214
  237.1 44.3 %expert_second.7 = bf16[32,96,2048]{2,1,0:T(8,128)(2,1)} custom-call(s32[1]{0:T(128)} %constant.193.clone.1.sel_ref, s32[2,32,512]{2,1,0:T(8,128)} %pad_add_fusion.slot_ref, bf16[32,512,512]{2,1,0:T(8,128)(2,1)} %bitcast.72, f32[2,1536,1408]{2,1,0:T(8,128)} %expert_first.7.acc_ref, bf16[2,2048,1408]{2,1,0:T(8,128)(2,1)} %w_ref.3, bf16[2,1408,2048]{2,1,0:T(8,128)(2,1)} %v_ref.1), custom_call_target="tpu_custom_call" | custom-call | flops 23756537856 | bytes 61079552 | tf_op jit(solution)/shard_map/expert_second/pallas_call | solution.py:106
  281.4 6.6 conditional.9
  281.8 6.2 broadcast.71
  288.0 6.4 conditional.10
  288.0 6.3 broadcast.72
  294.4 0.1 reduce-scatter.3.cloned.1.call-update
  294.5 125.9 %all-to-all-start = ((bf16[32,96,2048]{2,1,0:T(8,128)(2,1)}), bf16[32,96,2048]{2,1,0:T(8,128)(2,1)}, u32[]{:S(2)}, u32[]{:S(2)}) async-start(bf16[32,96,2048]{2,1,0:T(8,128)(2,1)} %expert_second.7), calls=%async_computation.1 | async-start | bytes 25165824 | tf_op jit(solution)/shard_map/all_to_all | solution.py:270
  421.1 244.3 %conditional.11 = (bf16[96,2048]{1,0:T(8,128)(2,1)S(1)}) conditional(s32[]{:T(128)} %clamp.3, bf16[32,96,2048]{2,1,0:T(8,128)(2,1)} %get-tuple-element.687, bf16[32,96,2048]{2,1,0:T(8,128)(2,1)} %get-tuple-element.687, bf16[32,96,2048]{2,1,0:T(8,128)(2,1)} %get-tuple-element.687, ...), branch_computations={%region_20.21_spmd, %region_21.22_spmd, %region_22.23_spmd, %regio... | conditional | bytes 8 | solution.py:284
  421.1 244.0 %scatter_over.58 = bf16[96,2048]{1,0:T(8,128)(2,1)S(1)} custom-call(bf16[32,96,2048]{2,1,0:T(8,128)(2,1)} %rows_ref.26), custom_call_target="tpu_custom_call" | custom-call | tf_op jit(solution)/shard_map/cond/branch_26_fun/scatter_over/pallas_call | solution.py:176
  665.4 0.8 dynamic-slice_reduce_fusion.1
  666.2 0.8 dynamic-slice_add_fusion.1
  667.0 1.0 slice_convert_fusion
  668.0 2.7 fusion.64
  670.7 6.4 add_add_fusion
  677.2 0.0 all-to-all-done
  677.2 11.9 %combine.1 = bf16[512,2048]{1,0:T(8,128)(2,1)} custom-call(bf16[512,3072]{1,0:T(8,128)(2,1)} %fusion.28.comb_ref, bf16[3072,2048]{1,0:T(8,128)(2,1)} %bitcast.14.back_ref, f32[512,2048]{1,0:T(8,128)} %get-tuple-element.467.part_ref), custom_call_target="tpu_custom_call" | custom-call | flops 6442450944 | bytes 22020096 | tf_op jit(solution)/shard_map/combine/pallas_call | solution.py:133
  (14 shorter events, 0.1 us)
Async XLA Ops:
  6.5 6.7 copy-start.2
  6.5 6.6 copy-start.6
  6.6 161.5 %all-gather.5.cloned.1.call-start = ((), (), s32[]{:S(2)}) async-start(), calls=%async_computation.4 | async-start | bytes 53526528 | tf_op jit(solution)/shard_map/all_gather | solution.py:213
  11.1 226.0 %all-gather.7.cloned.1.call-start = ((), (), s32[]{:S(2)}) async-start(), calls=%async_computation.5 | async-start | bytes 17301504 | tf_op jit(solution)/shard_map/all_gather | solution.py:214
  13.1 657.6 %reduce-scatter.3.cloned.1.call-start = ((), (), s32[]{:S(2)}) async-start(), calls=%async_computation.3 | async-start | bytes 12976128 | tf_op jit(solution)/shard_map/reduce_scatter | solution.py:287
  13.3 0.6 copy-start.1
  17.6 3.5 copy-start.3
  21.1 7.6 %copy-start = (bf16[3072,512]{0,1:T(8,128)(2,1)S(1)}, bf16[3072,512]{0,1:T(8,128)(2,1)}, u32[]{:S(2)}) copy-start(bf16[3072,512]{0,1:T(8,128)(2,1)} %copy.13) | copy-start | bytes 9437188
  169.0 1.4 copy-start.7
  169.1 0.6 copy-start.4
  294.5 382.7 %all-to-all-start = ((bf16[32,96,2048]{2,1,0:T(8,128)(2,1)}), bf16[32,96,2048]{2,1,0:T(8,128)(2,1)}, u32[]{:S(2)}, u32[]{:S(2)}) async-start(bf16[32,96,2048]{2,1,0:T(8,128)(2,1)} %expert_second.7), calls=%async_computation.1 | async-start | bytes 25165824 | tf_op jit(solution)/shard_map/all_to_all | solution.py:270
  670.7 6.5 copy-start.5
  670.7 6.5 copy-start.8
Sparse Core Ops, SparseCore 0:
  11.2 156.8 all-gather.4
  170.2 66.8 all-gather.6
  294.6 313.6 reduce-scatter.2
where the time goes:
time: 699 us; the launch traced here: 696 us
  Pallas kernels  337 us (48%)
  starting transfers between devices  126 us (18%)
  waiting for transfers between devices  121 us (17%)
  local copies, waits for them, and re-layouts  47.4 us (7%)
  matrix products  32.9 us (5%)
  between operations  17 us (2%)
  other arithmetic  13.7 us (2%)
    pallas_call x1, Pallas kernels, scatter_from(): pl.pallas_call(functools.partial(scatter_kernel, owner, axis, size), out_...  244 us
    all_to_all x1, starting transfers between devices, local_layer(): lax.all_to_all(out, 'ep', 0, 0, tiled=True)  126 us
    all_gather x1, waiting for transfers between devices, local_layer(): lax.all_gather(jnp.concatenate([x_loc[:, :cut], meta], axis=0), 'ep')  111 us
    pallas_call x1, Pallas kernels, expert_second(): pl.pallas_call(functools.partial(second_kernel, cap), out_shape=jax.Shape...  44.3 us
    pallas_call x1, Pallas kernels, expert_first(): pl.pallas_call(functools.partial(first_kernel, cap), out_shape=jax.ShapeD...  36.8 us
    another operation x4, local copies, waits for them, and re-layouts  27 us
    dot_general x1, matrix products, local_layer(): jnp.dot(shared_hidden, shared_out, preferred_element_type=jnp.float32)  22.7 us
  transfers between devices with their start and end apart: 4, of which 2 were waited for; matrix products, arithmetic and copies ran while one was open for 11% of the time, Pallas kernels for 40%

commit v1 on v0

--- a/solution.py
+++ b/solution.py
@@ -52,7 +52,7 @@
 
     gather_rows(slot_ref, x_ref, cap, put)
     for g in range(w_ref.shape[0]):
-        pre = acc_ref[g] + jnp.dot(rows_ref[g], w_ref[g], preferred_element_type=jnp.float32)
+        pre = acc_ref[g] + jnp.dot(rows_ref[g], w_ref[g, -rows_ref.shape[2]:], preferred_element_type=jnp.float32)
         hid = gelu(pre).astype(jnp.bfloat16)
         out = jnp.dot(hid, v_ref[g], preferred_element_type=jnp.float32).astype(jnp.bfloat16)
         out_ref[:, g * cap:(g + 1) * cap] = out.reshape(out_ref.shape[0], cap, out_ref.shape[2])
@@ -102,7 +102,7 @@
 def expert_second(sel, slots, x_part, acc, w_in, w_out, cap):
     groups, srcs, toks = slots.shape
     width, ff, model, blk = x_part.shape[2], w_out.shape[1], w_out.shape[2], SRC_BLOCK
-    last = w_in.shape[1] // width - 1
+    cut = w_in.shape[1] - width
     return pl.pallas_call(
         functools.partial(second_kernel, cap),
         out_shape=jax.ShapeDtypeStruct((srcs, groups * cap, model), jnp.bfloat16),
@@ -113,7 +113,7 @@
                 pl.BlockSpec((groups, blk, toks), lambda i, sel: (0, i, 0)),
                 pl.BlockSpec((blk, toks, width), lambda i, sel: (i, 0, 0)),
                 pl.BlockSpec((groups, blk * cap, ff), lambda i, sel: (0, i, 0)),
-                once((groups, width, ff), lambda i, sel: (sel[0], last, 0)),
+                once((groups, cut + width, ff), lambda i, sel: (sel[0], 0, 0)),
                 once((groups, ff, model), lambda i, sel: (sel[0], 0, 0)),
             ],
             out_specs=pl.BlockSpec((blk, groups * cap, model), lambda i, sel: (i, 0, 0)),
@@ -146,40 +146,84 @@
     )(comb, back, part)
 
 
-def scatter_kernel(owner, axis, size, rows_ref, out_ref, local_sem, send_sem, recv_sem):
+def scatter_kernel(owner, axis, size, rows_ref, out_ref, relay_ref, local_sem, send_sem, hand_sem, land_sem, recv_sem):
     me = lax.axis_index(axis)
+    core, partner, chips = owner % 2, owner + 1 - 2 * (owner % 2), size // 2
+    stride = next(n for n in range(chips // 3 | 1, 2 * chips) if math.gcd(n, chips) == 1)
     barrier = pltpu.get_barrier_semaphore()
-    stride = next(n for n in range(size // 3 | 1, 2 * size) if math.gcd(n, size) == 1)
-
-    def send_to(k):
-        dst = lax.rem(owner + k * stride, size)
+
+    def remote(src, dst, send, recv, device):
         return pltpu.make_async_remote_copy(
-            src_ref=rows_ref.at[dst], dst_ref=out_ref, send_sem=send_sem.at[k], recv_sem=recv_sem,
-            device_id={axis: dst}, device_id_type=pl.DeviceIdType.MESH)
-
-    @pl.when(me != owner)
-    def _():
-        pl.semaphore_signal(barrier, inc=1, device_id={axis: owner}, device_id_type=pl.DeviceIdType.MESH)
-        send_to(0).wait_recv()
+            src_ref=src, dst_ref=dst, send_sem=send, recv_sem=recv,
+            device_id={axis: device}, device_id_type=pl.DeviceIdType.MESH)
+
+    def target(k, on_core):
+        return 2 * lax.rem(owner // 2 + k * stride, chips) + on_core
+
+    def direct(k):
+        dst = target(k, core)
+        return remote(rows_ref.at[dst], out_ref, send_sem.at[k], recv_sem, dst)
+
+    def hand(k):
+        return remote(rows_ref.at[target(k, 1 - core)], relay_ref.at[k], hand_sem.at[k], land_sem.at[k], partner)
+
+    def forward(k):
+        return remote(relay_ref.at[k], out_ref, send_sem.at[k], recv_sem, target(k, 1 - core))
+
+    to_partner = remote(rows_ref.at[partner], out_ref, send_sem.at[0], recv_sem, partner)
+
+    def each(act):
+        lax.fori_loop(1, chips, lambda k, c: (act(k), c)[1], 0)
+
+    def tell(device):
+        pl.semaphore_signal(barrier, inc=1, device_id={axis: device}, device_id_type=pl.DeviceIdType.MESH)
 
     @pl.when(me == owner)
     def _():
-        own = pltpu.make_async_copy(rows_ref.at[owner], out_ref, local_sem)
-        own.start()
+        mine = pltpu.make_async_copy(rows_ref.at[owner], out_ref, local_sem)
+        mine.start()
         pl.semaphore_wait(barrier, size - 1)
-        lax.fori_loop(1, size, lambda k, c: (send_to(k).start(), c)[1], 0)
-        lax.fori_loop(1, size, lambda k, c: (send_to(k).wait_send(), c)[1], 0)
-        own.wait()
-
-
-def scatter_from(owner, axis, size, ident, rows):
+        each(lambda k: hand(k).start())
+        each(lambda k: direct(k).start())
+        to_partner.start()
+        each(lambda k: hand(k).wait_send())
+        each(lambda k: direct(k).wait_send())
+        to_partner.wait_send()
+        mine.wait()
+
+    @pl.when(me == partner)
+    def _():
+        tell(owner)
+        pl.semaphore_wait(barrier, size - 2)
+
+        def pass_on(k):
+            hand(k).wait_recv()
+            forward(k).start()
+
+        each(pass_on)
+        each(lambda k: forward(k).wait_send())
+        to_partner.wait_recv()
+
+    @pl.when((me != owner) & (me != partner))
+    def _():
+        tell(owner)
+        tell(partner)
+        to_partner.wait_recv()
+
+
+def scatter_from(owner, axis, size, rows):
+    chips = size // 2
     return pl.pallas_call(
         functools.partial(scatter_kernel, owner, axis, size),
         out_shape=jax.ShapeDtypeStruct(rows.shape[1:], rows.dtype),
-        in_specs=[pl.BlockSpec(memory_space=pltpu.VMEM)],
+        in_specs=[pl.BlockSpec(memory_space=pl.ANY)],
         out_specs=pl.BlockSpec(memory_space=pl.ANY),
-        scratch_shapes=[pltpu.SemaphoreType.DMA, pltpu.SemaphoreType.DMA((size,)), pltpu.SemaphoreType.DMA],
-        compiler_params=pltpu.CompilerParams(collective_id=ident, has_side_effects=True, vmem_limit_bytes=32 * 2 ** 20),
+        scratch_shapes=[
+            pltpu.VMEM((chips,) + rows.shape[1:], rows.dtype),
+            pltpu.SemaphoreType.DMA, pltpu.SemaphoreType.DMA((chips,)), pltpu.SemaphoreType.DMA((chips,)),
+            pltpu.SemaphoreType.DMA((chips,)), pltpu.SemaphoreType.DMA,
+        ],
+        compiler_params=pltpu.CompilerParams(collective_id=0, has_side_effects=True, vmem_limit_bytes=16 * 2 ** 20),
         name="scatter_over",
     )(rows)
 
@@ -195,7 +239,7 @@
         slot_cap = min(tok_rows, LOAD_MULT * tok_rows * top_k // num_experts)
         cap = BASE_CAP
         over_cap = slot_cap - cap
-        cut = model * 3 // 4
+        cut = model * 5 // 8
         me = lax.axis_index('ep')
         experts = jnp.arange(num_experts, dtype=jnp.int32)
 
@@ -281,7 +325,7 @@
 
         def scatter(setup, rows):
             owner = jnp.minimum(setup[0], num_experts - 1) // own
-            return lax.switch(owner, [functools.partial(scatter_from, d, 'ep', group_size, 0) for d in range(group_size)], rows)
+            return lax.switch(owner, [functools.partial(scatter_from, d, 'ep', group_size) for d in range(group_size)], rows)
 
         def spread(rows):
             return lax.psum_scatter(rows.reshape(group_size * over_cap, model), 'ep', scatter_dimension=0, tiled=True)

time: 699 us -> 681 us (0.974)
  the two profiles are of different devices: /device:TPU:111 before, /device:TPU:112 now
where the time goes in v1:
time: 681 us; the launch traced here: 678 us
  Pallas kernels  340 us (50%)
  waiting for transfers between devices  121 us (18%)
  starting transfers between devices  103 us (15%)
  local copies, waits for them, and re-layouts  48.2 us (7%)
  matrix products  33.4 us (5%)
  between operations  17 us (2%)
  other arithmetic  13.6 us (2%)
    pallas_call x1, Pallas kernels, scatter_from(): pl.pallas_call(functools.partial(scatter_kernel, owner, axis, size), out_...  245 us
    all_to_all x1, starting transfers between devices, local_layer(): lax.all_to_all(out, 'ep', 0, 0, tiled=True)  103 us
    all_gather x1, waiting for transfers between devices, local_layer(): lax.all_gather(jnp.concatenate([x_loc[:, :cut], meta], axis=0), 'ep')  88.1 us
    pallas_call x1, Pallas kernels, expert_second(): pl.pallas_call(functools.partial(second_kernel, cap), out_shape=jax.Shape...  51 us
    all_gather x1, waiting for transfers between devices, local_layer(): x_second = lax.all_gather(x_loc[:, cut:], 'ep')  33 us
    pallas_call x1, Pallas kernels, expert_first(): pl.pallas_call(functools.partial(first_kernel, cap), out_shape=jax.ShapeD...  32.3 us
    another operation x4, local copies, waits for them, and re-layouts  27.3 us
    dot_general x1, matrix products, local_layer(): jnp.dot(shared_hidden, shared_out, preferred_element_type=jnp.float32)  23.3 us
  transfers between devices with their start and end apart: 4, of which 2 were waited for; matrix products, arithmetic and copies ran while one was open for 11% of the time, Pallas kernels for 41%

profile of v1, /device:TPU:112, one launch (start us, length us, event | category | flops | bytes accessed | tf_op | source)
XLA Modules:
  0.0 678.0 jit_solution(15520558782233372585)
XLA Ops:
  6.6 0.0 all-gather.5.cloned.1.call-start
  6.6 0.8 bitcast_convert_fusion
  7.3 0.7 eq.174
  8.1 0.2 convert_reduce_fusion
  8.3 1.4 slice.12
  9.7 1.2 fusion.35
  10.8 0.1 all-gather.5.cloned.1.call-update
  10.9 0.1 all-gather.7.cloned.1.call-start
  11.0 2.1 slice.14
  13.0 0.1 all-gather.7.cloned.1.call-update
  13.1 0.1 reduce-scatter.3.cloned.1.call-start
  13.2 0.0 copy-done.6
  13.2 0.0 copy-done.2
  13.2 0.1 fusion.58
  13.3 0.0 copy-start.1
  13.3 0.6 copy-done.1
  13.9 0.2 broadcast_in_dim.127
  14.2 3.1 copy.13
  17.2 0.1 fusion.53
  17.3 0.2 fusion.37
  17.6 0.0 copy-start.3
  17.6 3.7 eq.181
  21.3 0.0 copy-done.3
  21.3 7.7 %copy.12 = s32[3072,512]{0,1:T(8,128)} copy(s32[3072,512]{1,0:T(8,128)} %bitcast.64) | data formatting | bytes 12582912 | tf_op jit(solution)/shard_map/eq | solution.py:266
  28.9 0.1 eq.184
  29.0 0.0 copy-done
  29.0 5.3 fusion.27.comb_ref
  34.3 23.3 %fusion.28 = f32[512,2048]{1,0:T(8,128)} fusion(bf16[2816,2048]{1,0:T(8,128)(2,1)} %param.59, bf16[512,2048]{1,0:T(8,128)(2,1)} %param.53, bf16[2048,2816]{1,0:T(8,128)(2,1)} %param.58), kind=kOutput, calls=%fused_computation.35 | convolution fusion | flops 11824136192 | bytes 29360128 | tf_op jit(solution)/shard_map/dot_general | solution.py:273
  57.6 88.1 %all-gather.5.cloned.1.call-done = bf16[16896,1280]{1,0:T(8,128)(2,1)} async-done(((bf16[528,1280]{1,0:T(8,128)(2,1)}), bf16[16896,1280]{1,0:T(8,128)(2,1)}) %all-gather.5.cloned.1.call-update) | async-done | bytes 43253776 | tf_op jit(solution)/shard_map/all_gather | solution.py:257
  145.7 0.9 convert_reduce_fusion.2
  146.6 0.0 copy-start.7
  146.6 0.1 convert_reduce_fusion.1
  146.7 0.0 copy-start.4
  146.7 0.5 copy-done.4
  147.3 0.7 fusion.78
  148.0 0.0 copy-done.7
  150.7 1.7 fusion.57
  152.5 0.2 fusion.49
  152.7 0.2 fusion.51
  152.9 7.7 %conditional.7 = (f32[1,3072,1408]{2,1,0:T(8,128)}) conditional(s32[]{:T(128)} %convert_element_type.95, () %tuple.157, (s32[1]{0:T(128)}, s32[1,32,512]{2,1,0:T(8,128)S(1)}, bf16[32,528,1280]{2,1,0:T(8,128)(2,1)}, bf16[2,2048,1408]{2,1,0:T(8,128)(2,1)}) %tuple.254), branch_computations={%region_10.11_spmd, %region_11.12_spmd} | conditional | flops 15099494400 | bytes 62849032 | solution.py:297
  152.9 7.6 %broadcast.69 = f32[1,3072,1408]{2,1,0:T(8,128)} broadcast(f32[]{:T(128)} %constant.170.clone), dimensions={} | broadcast | bytes 17301508 | tf_op jit(solution)/shard_map/broadcast.4
  160.6 7.2 %conditional.8 = (f32[1,3072,1408]{2,1,0:T(8,128)}) conditional(s32[]{:T(128)} %convert_element_type.97, () %tuple.159, (s32[1]{0:T(128)}, s32[1,32,512]{2,1,0:T(8,128)S(1)}, bf16[32,528,1280]{2,1,0:T(8,128)(2,1)}, bf16[2,2048,1408]{2,1,0:T(8,128)(2,1)}) %tuple.255), branch_computations={%region_14.15_spmd, %region_15.16_spmd} | conditional | flops 15099494400 | bytes 62849032 | solution.py:297
  160.6 7.2 %broadcast.70 = f32[1,3072,1408]{2,1,0:T(8,128)} broadcast(f32[]{:T(128)} %constant.171.clone), dimensions={} | broadcast | bytes 17301508 | tf_op jit(solution)/shard_map/broadcast.6
  167.8 0.2 fusion.44
  168.0 0.2 fusion.47
  168.2 0.7 pad_add_fusion.slot_ref
  168.9 32.3 %expert_first.7.acc_ref = f32[2,1536,1408]{2,1,0:T(8,128)} custom-call(s32[1]{0:T(128)} %constant.193.clone.1.sel_ref, s32[2,32,512]{2,1,0:T(8,128)} %pad_add_fusion.slot_ref, bf16[32,528,1280]{2,1,0:T(8,128)(2,1)} %bitcast.59, bf16[2,2048,1408]{2,1,0:T(8,128)(2,1)} %w_ref.3), custom_call_target="tpu_custom_call" | custom-call | flops 15099494400 | bytes 66453504 | tf_op jit(solution)/shard_map/expert_first/pallas_call | solution.py:81
  201.2 33.0 %all-gather.7.cloned.1.call-done = bf16[16384,768]{1,0:T(8,128)(2,1)} async-done(((bf16[512,768]{1,0:T(8,128)(2,1)}), bf16[16384,768]{1,0:T(8,128)(2,1)}) %all-gather.7.cloned.1.call-update) | async-done | bytes 25165840 | tf_op jit(solution)/shard_map/all_gather | solution.py:258
  234.1 51.0 %expert_second.7 = bf16[32,96,2048]{2,1,0:T(8,128)(2,1)} custom-call(s32[1]{0:T(128)} %constant.193.clone.1.sel_ref, s32[2,32,512]{2,1,0:T(8,128)} %pad_add_fusion.slot_ref, bf16[32,512,768]{2,1,0:T(8,128)(2,1)} %bitcast.72, f32[2,1536,1408]{2,1,0:T(8,128)} %expert_first.7.acc_ref, bf16[2,2048,1408]{2,1,0:T(8,128)(2,1)} %w_ref.3, bf16[2,1408,2048]{2,1,0:T(8,128)(2,1)} %v_ref.1), custom_call_target="tpu_custom_call" | custom-call | flops 26776436736 | bytes 70909952 | tf_op jit(solution)/shard_map/expert_second/pallas_call | solution.py:106
  285.1 6.5 conditional.9
  285.3 6.3 broadcast.71
  291.6 6.7 conditional.10
  291.6 6.2 broadcast.72
  298.3 0.1 reduce-scatter.3.cloned.1.call-update
  298.3 103.0 %all-to-all-start = ((bf16[32,96,2048]{2,1,0:T(8,128)(2,1)}), bf16[32,96,2048]{2,1,0:T(8,128)(2,1)}, u32[]{:S(2)}, u32[]{:S(2)}) async-start(bf16[32,96,2048]{2,1,0:T(8,128)(2,1)} %expert_second.7), calls=%async_computation.1 | async-start | bytes 25165824 | tf_op jit(solution)/shard_map/all_to_all | solution.py:314
  402.1 245.6 %conditional.11 = (bf16[96,2048]{1,0:T(8,128)(2,1)S(1)}) conditional(s32[]{:T(128)} %clamp.3, bf16[32,96,2048]{2,1,0:T(8,128)(2,1)} %get-tuple-element.687, bf16[32,96,2048]{2,1,0:T(8,128)(2,1)} %get-tuple-element.687, bf16[32,96,2048]{2,1,0:T(8,128)(2,1)} %get-tuple-element.687, ...), branch_computations={%region_20.21_spmd, %region_21.22_spmd, %region_22.23_spmd, %regio... | conditional | bytes 8 | solution.py:328
  402.1 245.3 %scatter_over.58 = bf16[96,2048]{1,0:T(8,128)(2,1)S(1)} custom-call(bf16[32,96,2048]{2,1,0:T(8,128)(2,1)} %rows_ref.26), custom_call_target="tpu_custom_call" | custom-call | tf_op jit(solution)/shard_map/cond/branch_26_fun/scatter_over/pallas_call | solution.py:216
  647.7 0.8 dynamic-slice_reduce_fusion.1
  648.5 0.8 dynamic-slice_add_fusion.1
  649.3 1.0 slice_convert_fusion
  650.3 2.7 fusion.64
  653.0 6.4 add_add_fusion
  659.3 0.0 all-to-all-done
  659.4 11.9 %combine.1 = bf16[512,2048]{1,0:T(8,128)(2,1)} custom-call(bf16[512,3072]{1,0:T(8,128)(2,1)} %fusion.27.comb_ref, bf16[3072,2048]{1,0:T(8,128)(2,1)} %bitcast.14.back_ref, f32[512,2048]{1,0:T(8,128)} %get-tuple-element.467.part_ref), custom_call_target="tpu_custom_call" | custom-call | flops 6442450944 | bytes 22020096 | tf_op jit(solution)/shard_map/combine/pallas_call | solution.py:133
  (14 shorter events, 0.1 us)
Async XLA Ops:
  6.5 6.6 copy-start.2
  6.5 6.6 copy-start.6
  6.6 139.1 %all-gather.5.cloned.1.call-start = ((), (), s32[]{:S(2)}) async-start(), calls=%async_computation.4 | async-start | bytes 44605440 | tf_op jit(solution)/shard_map/all_gather | solution.py:257
  10.9 223.2 %all-gather.7.cloned.1.call-start = ((), (), s32[]{:S(2)}) async-start(), calls=%async_computation.5 | async-start | bytes 25952256 | tf_op jit(solution)/shard_map/all_gather | solution.py:258
  13.1 639.9 %reduce-scatter.3.cloned.1.call-start = ((), (), s32[]{:S(2)}) async-start(), calls=%async_computation.3 | async-start | bytes 12976128 | tf_op jit(solution)/shard_map/reduce_scatter | solution.py:331
  13.3 0.6 copy-start.1
  17.6 3.7 copy-start.3
  21.3 7.8 %copy-start = (bf16[3072,512]{0,1:T(8,128)(2,1)S(1)}, bf16[3072,512]{0,1:T(8,128)(2,1)}, u32[]{:S(2)}) copy-start(bf16[3072,512]{0,1:T(8,128)(2,1)} %copy.13) | copy-start | bytes 9437188
  146.6 1.4 copy-start.7
  146.7 0.5 copy-start.4
  298.3 361.0 %all-to-all-start = ((bf16[32,96,2048]{2,1,0:T(8,128)(2,1)}), bf16[32,96,2048]{2,1,0:T(8,128)(2,1)}, u32[]{:S(2)}, u32[]{:S(2)}) async-start(bf16[32,96,2048]{2,1,0:T(8,128)(2,1)} %expert_second.7), calls=%async_computation.1 | async-start | bytes 25165824 | tf_op jit(solution)/shard_map/all_to_all | solution.py:314
  653.0 6.4 copy-start.5
  653.0 6.4 copy-start.8
Sparse Core Ops, SparseCore 0:
  11.0 134.6 all-gather.4
  147.8 86.3 all-gather.6
  298.5 297.6 reduce-scatter.2

commit v2 on v1

--- a/solution.py
+++ b/solution.py
@@ -58,9 +58,12 @@
         out_ref[:, g * cap:(g + 1) * cap] = out.reshape(out_ref.shape[0], cap, out_ref.shape[2])
 
 
-def combine_kernel(comb_ref, back_ref, part_ref, out_ref):
-    routed = jnp.dot(comb_ref[...], back_ref[...], preferred_element_type=jnp.float32)
-    out_ref[...] = (part_ref[...] + routed).astype(out_ref.dtype)
+def combine_kernel(*refs):
+    part_ref, out_ref = refs[-2:]
+    total = part_ref[...]
+    for comb_ref, back_ref in zip(refs[:-2:2], refs[1:-2:2]):
+        total = total + jnp.dot(comb_ref[...], back_ref[...], preferred_element_type=jnp.float32)
+    out_ref[...] = total.astype(out_ref.dtype)
 
 
 def params():
@@ -127,23 +130,23 @@
     )(sel, slots, x_part, acc, w_in, w_out)
 
 
-def combine(comb, back, part):
-    toks, pairs = comb.shape
-    model, blk = back.shape[1], COMBINE_BLOCK
+def combine(pairs, part):
+    toks, model = part.shape
+    blk = COMBINE_BLOCK
+    depth = sum(rows.shape[0] for _, rows in pairs)
+    specs = []
+    for comb, rows in pairs:
+        specs += [once(comb.shape, lambda i: (0, 0)), pl.BlockSpec((rows.shape[0], blk), lambda i: (0, i))]
     return pl.pallas_call(
         combine_kernel,
         out_shape=jax.ShapeDtypeStruct((toks, model), jnp.bfloat16),
         grid=(model // blk,),
-        in_specs=[
-            once((toks, pairs), lambda i: (0, 0)),
-            pl.BlockSpec((pairs, blk), lambda i: (0, i)),
-            pl.BlockSpec((toks, blk), lambda i: (0, i)),
-        ],
+        in_specs=specs + [pl.BlockSpec((toks, blk), lambda i: (0, i))],
         out_specs=pl.BlockSpec((toks, blk), lambda i: (0, i)),
         compiler_params=params(),
-        cost_estimate=cost(2 * toks * pairs * model, pairs * (toks + model) * 2 + toks * model * 6),
+        cost_estimate=cost(2 * toks * depth * model, depth * (toks + model) * 2 + toks * model * 6),
         name="combine",
-    )(comb, back, part)
+    )(*[ref for pair in pairs for ref in pair], part)
 
 
 def scatter_kernel(owner, axis, size, rows_ref, out_ref, relay_ref, local_sem, send_sem, hand_sem, land_sem, recv_sem):
@@ -266,9 +269,6 @@
         pick = slot_loc[:, None, :] == jnp.arange(cap, dtype=jnp.int32)[None, :, None]
         comb = jnp.where(pick, gate_of[:, None, :], 0).astype(jnp.bfloat16).reshape(num_experts * cap, tok_rows).T
 
-        def weigh(comb, rows):
-            return lax.dot_general(comb, rows, (((0,), (0,)), ((), ())), preferred_element_type=jnp.float32)
-
         shared_hidden = gelu(jnp.dot(x_loc, shared_in, preferred_element_type=jnp.float32)).astype(jnp.bfloat16)
         shared_val = jnp.dot(shared_hidden, shared_out, preferred_element_type=jnp.float32)
         x_first, shared_val, comb = lax.optimization_barrier((x_first, shared_val, comb))
@@ -316,12 +316,12 @@
         over_outs = [over_second(s, x_over, a) for s, a in zip(setups, over_accs)]
         over_outs = lax.optimization_barrier(over_outs)
 
-        def over_combine(expert, rows):
+        def over_table(expert):
             at = jnp.minimum(expert, num_experts - 1)
             slot = lax.dynamic_index_in_dim(slot_loc, at, 0, keepdims=True)
             gate = lax.dynamic_index_in_dim(gate_of, at, 0, keepdims=True)
             pick = (slot - cap == lax.broadcasted_iota(jnp.int32, (over_cap, tok_rows), 0)) & (expert < num_experts)
-            return weigh(jnp.where(pick, gate, 0).astype(jnp.bfloat16), rows)
+            return jnp.where(pick, gate, 0).astype(jnp.bfloat16).T
 
         def scatter(setup, rows):
             owner = jnp.minimum(setup[0], num_experts - 1) // own
@@ -331,16 +331,18 @@
             return lax.psum_scatter(rows.reshape(group_size * over_cap, model), 'ep', scatter_dimension=0, tiled=True)
 
         rest = [spread(rows) for rows in over_outs[1:]]
-        total = shared_val + over_combine(setups[0][0], scatter(setups[0], over_outs[0]))
-        for setup, rows in zip(setups[1:], rest):
-            total = total + over_combine(setup[0], rows)
+        tables = [over_table(setup[0]) for setup in setups]
 
         def more(i, total):
             setup = over_setup(i)
-            return total + over_combine(setup[0], spread(over_second(setup, x_over, over_first(setup, x_first))))
-
+            rows = spread(over_second(setup, x_over, over_first(setup, x_first)))
+            return total + jnp.dot(over_table(setup[0]), rows, preferred_element_type=jnp.float32)
+
+        first, tables = lax.optimization_barrier((over_outs[0], tables))
+        sent = scatter(setups[0], first)
+        sent, rest, total = lax.optimization_barrier((sent, rest, shared_val))
         total = lax.fori_loop(HOT_STATIC, jnp.maximum(num_over, HOT_STATIC), more, total)
-        return combine(comb, back, total)
+        return combine([(comb, back)] + list(zip(tables, [sent] + rest)), total)
 
     tok_spec = P(('dp', 'ep'), None)
     expert_spec = P('ep', None, None)

time: 681 us -> 674 us (0.990)
  matrix products: 33.4 us -> 24.5 us
    dot_general x2 -> x0, matrix products: 9.04 us -> none  [weigh(): lax.dot_general(comb, rows, (((0,), (0,)), ((), ())), preferred_element_t...]
  transfers between devices with their start and end apart: 4 -> 4, of which waited for: 2 -> 2; matrix products, arithmetic and copies ran while one was open for 11% -> 10% of each run, Pallas kernels for 41% -> 41%
where the time goes in v2:
time: 674 us; the launch traced here: 670 us
  Pallas kernels  339 us (50%)
  waiting for transfers between devices  121 us (18%)
  starting transfers between devices  103 us (15%)
  local copies, waits for them, and re-layouts  49.6 us (7%)
  matrix products  24.5 us (4%)
  between operations  17.3 us (3%)
  other arithmetic  14.6 us (2%)
    pallas_call x1, Pallas kernels, scatter_from(): pl.pallas_call(functools.partial(scatter_kernel, owner, axis, size), out_...  243 us
    all_to_all x1, starting transfers between devices, local_layer(): lax.all_to_all(out, 'ep', 0, 0, tiled=True)  103 us
    all_gather x1, waiting for transfers between devices, local_layer(): lax.all_gather(jnp.concatenate([x_loc[:, :cut], meta], axis=0), 'ep')  88.2 us
    pallas_call x1, Pallas kernels, expert_second(): pl.pallas_call(functools.partial(second_kernel, cap), out_shape=jax.Shape...  51 us
    all_gather x1, waiting for transfers between devices, local_layer(): x_second = lax.all_gather(x_loc[:, cut:], 'ep')  32.7 us
    pallas_call x1, Pallas kernels, expert_first(): pl.pallas_call(functools.partial(first_kernel, cap), out_shape=jax.ShapeD...  32.2 us
    another operation x4, local copies, waits for them, and re-layouts  27.3 us
    dot_general x1, matrix products, local_layer(): jnp.dot(shared_hidden, shared_out, preferred_element_type=jnp.float32)  23.5 us
  transfers between devices with their start and end apart: 4, of which 2 were waited for; matrix products, arithmetic and copies ran while one was open for 10% of the time, Pallas kernels for 41%

profile of v2, /device:TPU:112, one launch (start us, length us, event | category | flops | bytes accessed | tf_op | source)
XLA Modules:
  0.0 670.3 jit_solution(8423685878170791176)
XLA Ops:
  6.6 0.0 all-gather.5.cloned.1.call-start
  6.6 0.8 bitcast_convert_fusion
  7.3 0.7 eq.176
  8.1 0.2 convert_reduce_fusion
  8.3 1.4 slice.12
  9.7 1.2 fusion.35
  10.8 0.1 all-gather.5.cloned.1.call-update
  10.9 0.1 all-gather.7.cloned.1.call-start
  11.0 2.1 slice.14
  13.0 0.1 all-gather.7.cloned.1.call-update
  13.1 0.1 reduce-scatter.3.cloned.1.call-start
  13.2 0.0 copy-done.8
  13.2 0.0 copy-done.4
  13.2 0.1 fusion.58
  13.3 0.0 copy-start.3
  13.3 0.6 copy-done.3
  13.9 0.2 broadcast_in_dim.127
  14.2 3.1 copy.13
  17.2 0.1 fusion.53
  17.3 0.2 fusion.37
  17.6 3.7 eq.183
  21.3 0.0 copy-done.5
  21.3 7.4 %copy.12 = s32[3072,512]{0,1:T(8,128)} copy(s32[3072,512]{1,0:T(8,128)} %bitcast.62) | data formatting | bytes 12582912 | tf_op jit(solution)/shard_map/eq | solution.py:269
  28.7 0.1 eq.186
  28.8 5.3 fusion.27.refs_0_
  34.0 23.5 %fusion.28 = f32[512,2048]{1,0:T(8,128)} fusion(bf16[2816,2048]{1,0:T(8,128)(2,1)} %param.59, bf16[512,2048]{1,0:T(8,128)(2,1)} %param.53, bf16[2048,2816]{1,0:T(8,128)(2,1)} %param.58), kind=kOutput, calls=%fused_computation.34 | convolution fusion | flops 11824136192 | bytes 29360128 | tf_op jit(solution)/shard_map/dot_general | solution.py:273
  57.5 88.2 %all-gather.5.cloned.1.call-done = bf16[16896,1280]{1,0:T(8,128)(2,1)} async-done(((bf16[528,1280]{1,0:T(8,128)(2,1)}), bf16[16896,1280]{1,0:T(8,128)(2,1)}) %all-gather.5.cloned.1.call-update) | async-done | bytes 43253776 | tf_op jit(solution)/shard_map/all_gather | solution.py:260
  145.7 0.9 convert_reduce_fusion.2
  146.6 0.0 copy-start.9
  146.6 0.1 convert_reduce_fusion.1
  146.7 0.5 copy-done.6
  147.2 0.7 fusion.67
  150.7 1.7 fusion.57
  152.4 0.2 fusion.49
  152.7 0.2 fusion.51
  152.9 8.0 %conditional.7 = (f32[1,3072,1408]{2,1,0:T(8,128)}) conditional(s32[]{:T(128)} %convert_element_type.95, () %tuple.159, (s32[1]{0:T(128)}, s32[1,32,512]{2,1,0:T(8,128)S(1)}, bf16[32,528,1280]{2,1,0:T(8,128)(2,1)}, bf16[2,2048,1408]{2,1,0:T(8,128)(2,1)}) %tuple.259), branch_computations={%region_10.11_spmd, %region_11.12_spmd} | conditional | flops 15099494400 | bytes 62849032 | solution.py:297
  152.9 7.6 %broadcast.77 = f32[1,3072,1408]{2,1,0:T(8,128)} broadcast(f32[]{:T(128)} %constant.170.clone), dimensions={} | broadcast | bytes 17301508 | tf_op jit(solution)/shard_map/broadcast.4
  160.8 7.2 %conditional.8 = (f32[1,3072,1408]{2,1,0:T(8,128)}) conditional(s32[]{:T(128)} %convert_element_type.97, () %tuple.161, (s32[1]{0:T(128)}, s32[1,32,512]{2,1,0:T(8,128)S(1)}, bf16[32,528,1280]{2,1,0:T(8,128)(2,1)}, bf16[2,2048,1408]{2,1,0:T(8,128)(2,1)}) %tuple.260), branch_computations={%region_14.15_spmd, %region_15.16_spmd} | conditional | flops 15099494400 | bytes 62849032 | solution.py:297
  160.9 7.2 %broadcast.78 = f32[1,3072,1408]{2,1,0:T(8,128)} broadcast(f32[]{:T(128)} %constant.171.clone), dimensions={} | broadcast | bytes 17301508 | tf_op jit(solution)/shard_map/broadcast.6
  168.1 0.2 fusion.44
  168.3 0.2 fusion.47
  168.5 0.7 pad_add_fusion.slot_ref
  169.2 32.2 %expert_first.7.acc_ref = f32[2,1536,1408]{2,1,0:T(8,128)} custom-call(s32[1]{0:T(128)} %constant.193.clone.1.sel_ref, s32[2,32,512]{2,1,0:T(8,128)} %pad_add_fusion.slot_ref, bf16[32,528,1280]{2,1,0:T(8,128)(2,1)} %bitcast.57, bf16[2,2048,1408]{2,1,0:T(8,128)(2,1)} %w_ref.3), custom_call_target="tpu_custom_call" | custom-call | flops 15099494400 | bytes 66453504 | tf_op jit(solution)/shard_map/expert_first/pallas_call | solution.py:84
  201.4 32.7 %all-gather.7.cloned.1.call-done = bf16[16384,768]{1,0:T(8,128)(2,1)} async-done(((bf16[512,768]{1,0:T(8,128)(2,1)}), bf16[16384,768]{1,0:T(8,128)(2,1)}) %all-gather.7.cloned.1.call-update) | async-done | bytes 25165840 | tf_op jit(solution)/shard_map/all_gather | solution.py:261
  234.1 51.0 %expert_second.7 = bf16[32,96,2048]{2,1,0:T(8,128)(2,1)} custom-call(s32[1]{0:T(128)} %constant.193.clone.1.sel_ref, s32[2,32,512]{2,1,0:T(8,128)} %pad_add_fusion.slot_ref, bf16[32,512,768]{2,1,0:T(8,128)(2,1)} %bitcast.70, f32[2,1536,1408]{2,1,0:T(8,128)} %expert_first.7.acc_ref, bf16[2,2048,1408]{2,1,0:T(8,128)(2,1)} %w_ref.3, bf16[2,1408,2048]{2,1,0:T(8,128)(2,1)} %v_ref.1), custom_call_target="tpu_custom_call" | custom-call | flops 26776436736 | bytes 70909952 | tf_op jit(solution)/shard_map/expert_second/pallas_call | solution.py:109
  285.1 6.4 conditional.9
  285.3 6.3 broadcast.79
  291.6 6.4 conditional.10
  291.6 6.2 broadcast.80
  298.0 0.1 reduce-scatter.3.cloned.1.call-update
  298.1 103.2 %all-to-all-start = ((bf16[32,96,2048]{2,1,0:T(8,128)(2,1)}), bf16[32,96,2048]{2,1,0:T(8,128)(2,1)}, u32[]{:S(2)}, u32[]{:S(2)}) async-start(bf16[32,96,2048]{2,1,0:T(8,128)(2,1)} %expert_second.7), calls=%async_computation.1 | async-start | bytes 25165824 | tf_op jit(solution)/shard_map/all_to_all | solution.py:314
  402.0 0.8 dynamic-slice_reduce_fusion.1
  402.8 0.8 dynamic-slice_add_fusion.1
  403.6 1.0 fusion.60
  404.7 243.0 %conditional.11 = (bf16[96,2048]{1,0:T(8,128)(2,1)S(1)}) conditional(s32[]{:T(128)} %clamp.3, bf16[32,96,2048]{2,1,0:T(8,128)(2,1)} %get-tuple-element.701, bf16[32,96,2048]{2,1,0:T(8,128)(2,1)} %get-tuple-element.701, bf16[32,96,2048]{2,1,0:T(8,128)(2,1)} %get-tuple-element.701, ...), branch_computations={%region_20.21_spmd, %region_21.22_spmd, %region_22.23_spmd, %regio... | conditional | bytes 8 | solution.py:328
  404.7 242.8 %scatter_over.58 = bf16[96,2048]{1,0:T(8,128)(2,1)S(1)} custom-call(bf16[32,96,2048]{2,1,0:T(8,128)(2,1)} %rows_ref.26), custom_call_target="tpu_custom_call" | custom-call | tf_op jit(solution)/shard_map/cond/branch_26_fun/scatter_over/pallas_call | solution.py:219
  647.7 0.0 copy-start.1
  647.7 0.7 copy-done.1
  648.4 1.0 slice_convert_fusion
  649.4 0.0 reduce-scatter.3.cloned.1.call-done.refs_5_
  649.5 0.0 all-to-all-done
  649.5 0.0 copy-start.2
  649.5 1.0 copy-done.2
  650.5 12.8 %combine.1 = bf16[512,2048]{1,0:T(8,128)(2,1)} custom-call(bf16[512,3072]{1,0:T(8,128)(2,1)} %fusion.27.refs_0_, bf16[3072,2048]{1,0:T(8,128)(2,1)} %bitcast.14.refs_1_, bf16[512,96]{1,0:T(8,128)(2,1)} %get-tuple-element.471.refs_2_, bf16[96,2048]{1,0:T(8,128)(2,1)S(1)} %copy-done.2, bf16[512,96]{1,0:T(8,128)(2,1)} %get-tuple-element.476.refs_4_, ...), custom_call_target="tpu_custom_call" | custom-call | flops 6845104128 | bytes 23003136 | tf_op jit(solution)/shard_map/combine/pallas_call | solution.py:140
  (17 shorter events, 0.1 us)
Async XLA Ops:
  6.5 6.6 copy-start.4
  6.5 6.6 copy-start.8
  6.6 139.1 %all-gather.5.cloned.1.call-start = ((), (), s32[]{:S(2)}) async-start(), calls=%async_computation.4 | async-start | bytes 44605440 | tf_op jit(solution)/shard_map/all_gather | solution.py:260
  10.9 223.2 %all-gather.7.cloned.1.call-start = ((), (), s32[]{:S(2)}) async-start(), calls=%async_computation.5 | async-start | bytes 25952256 | tf_op jit(solution)/shard_map/all_gather | solution.py:261
  13.1 636.4 %reduce-scatter.3.cloned.1.call-start = ((), (), s32[]{:S(2)}) async-start(), calls=%async_computation.3 | async-start | bytes 12976128 | tf_op jit(solution)/shard_map/reduce_scatter | solution.py:331
  13.3 0.6 copy-start.3
  17.6 3.7 copy-start.5
  21.3 7.5 %copy-start = (bf16[3072,512]{0,1:T(8,128)(2,1)S(1)}, bf16[3072,512]{0,1:T(8,128)(2,1)}, u32[]{:S(2)}) copy-start(bf16[3072,512]{0,1:T(8,128)(2,1)} %copy.13) | copy-start | bytes 9437188
  146.6 1.4 copy-start.9
  146.7 0.5 copy-start.6
  298.1 351.4 %all-to-all-start = ((bf16[32,96,2048]{2,1,0:T(8,128)(2,1)}), bf16[32,96,2048]{2,1,0:T(8,128)(2,1)}, u32[]{:S(2)}, u32[]{:S(2)}) async-start(bf16[32,96,2048]{2,1,0:T(8,128)(2,1)} %expert_second.7), calls=%async_computation.1 | async-start | bytes 25165824 | tf_op jit(solution)/shard_map/all_to_all | solution.py:314
  404.7 244.8 %copy-start.7 = (s32[64]{0:T(128)S(1)}, s32[64]{0:T(128)}, u32[]{:S(2)}) copy-start(s32[64]{0:T(128)} %copy-done.6) | copy-start | bytes 772
  404.7 244.8 %copy-start.10 = (pred[64]{0:T(512)(128)(4,1)S(1)}, pred[64]{0:T(512)(128)(4,1)}, u32[]{:S(2)}) copy-start(pred[64]{0:T(512)(128)(4,1)} %copy-done.9) | copy-start | bytes 196
  647.7 0.7 copy-start.1
  649.5 1.0 copy-start.2
Sparse Core Ops, SparseCore 0:
  11.0 134.6 all-gather.4
  147.8 86.3 all-gather.6
  298.2 297.7 reduce-scatter.2
